TPU v7x, 32 devices: a whole 2x2x4 slice. The times are simulated.
32 devices in a mesh: row: 4 (over z), col: 8 (over y, x, core).
Axes of the slice: x: 2, y: 2, z: 4, core: 2. Of those that a mesh axis runs over, the one named last changes fastest.
Arguments:
- hidden_in: bfloat16 [8192, 1536], P(('row', 'col')), may hold values from -6 to 6
- out_grad: bfloat16 [8192, 1536], P(('row', 'col')), may hold values from -6 to 6
- seq_lengths: int32 [4, 16], P('row'), may hold values from 1 to 1024, 2048 in all within a row
- norm1_gain: bfloat16 [1536], P(('row', 'col')), may hold values from 0.25 to 1.75
- q_weight: bfloat16 [1536, 1536], P('row', 'col'), may hold values from -0.15625 to 0.15625
- q_bias: bfloat16 [1536], P(('row', 'col')), may hold values from -3 to 3
- k_weight: bfloat16 [1536, 256], P('row', 'col'), may hold values from -0.15625 to 0.15625
- k_bias: bfloat16 [256], P(('row', 'col')), may hold values from -3 to 3
- v_weight: bfloat16 [1536, 256], P('row', 'col'), may hold values from -0.15625 to 0.15625
- v_bias: bfloat16 [256], P(('row', 'col')), may hold values from -3 to 3
- o_weight: bfloat16 [1536, 1536], P('row', 'col'), may hold values from -0.625 to 0.625
- norm2_gain: bfloat16 [1536], P(('row', 'col')), may hold values from 0.25 to 1.75
- gate_weight: bfloat16 [1536, 8960], P('row', 'col'), may hold values from -0.15625 to 0.15625
- up_weight: bfloat16 [1536, 8960], P('row', 'col'), may hold values from -0.15625 to 0.15625
- down_weight: bfloat16 [8960, 1536], P('col', 'row'), may hold values from -0.375 to 0.375
Outputs:
- layer_out: float32 [8192, 1536], P(('row', 'col'))
- input_grad: float32 [8192, 1536], P(('row', 'col'))
- norm1_gain_grad: float32 [1536], P(('row', 'col'))
- q_weight_grad: float32 [1536, 1536], P('row', 'col')
- q_bias_grad: float32 [1536], P(('row', 'col'))
- k_weight_grad: float32 [1536, 256], P('row', 'col')
- k_bias_grad: float32 [256], P(('row', 'col'))
- v_weight_grad: float32 [1536, 256], P('row', 'col')
- v_bias_grad: float32 [256], P(('row', 'col'))
- o_weight_grad: float32 [1536, 1536], P('row', 'col')
- norm2_gain_grad: float32 [1536], P(('row', 'col'))
- gate_weight_grad: float32 [1536, 8960], P('row', 'col')
- up_weight_grad: float32 [1536, 8960], P('row', 'col')
- down_weight_grad: float32 [8960, 1536], P('col', 'row')
Inputs may be any that keep to these rules, and one draw needn't show every extreme that they name: `seq_lengths`: row r lists the lengths of the 16 sequences packed in order into block r of 2048 tokens; they sum to 2048, and the longest is exactly 1024 in every row.
All inputs are finite; a program needn't handle non-finite values.
Results may differ from a plain program's by a relative error of at most 0.03.
Values may be sent and summed in bfloat16 or wider, within the bound.
A program may use at most 192 MiB of HBM per device.

v0:
```python
import math
import jax
import jax.numpy as jnp
from jax import lax
from jax.sharding import PartitionSpec as P

HQ = 12
KVH = 2
HD = 128
MAXLEN = 1024
EPSILON = 1e-06
ROPE_BASE = 1000000.0


def seq_starts(slots, lengths):
    bounds = jnp.cumsum(lengths)
    picked = jnp.where(bounds[None, :] <= slots[:, None], lengths[None, :], 0)
    return jnp.sum(picked, axis=1)


def rope_tables(positions, head_dim):
    steps_up = jnp.arange(head_dim // 2, dtype=jnp.float32)
    freqs = jnp.exp(-math.log(ROPE_BASE) * (2.0 * steps_up / head_dim))
    angles = positions.astype(jnp.float32)[:, None] * freqs[None, :]
    angles = jnp.concatenate([angles, angles], axis=1)
    return (jnp.cos(angles)[:, None, :], jnp.sin(angles)[:, None, :])


def rotate_pairs(values, cosines, sines):
    half_dim = values.shape[-1] // 2
    turned = jnp.concatenate([-values[..., half_dim:], values[..., :half_dim]], axis=-1)
    return values * cosines + turned * sines


def rotate_back(grads_in, cosines, sines):
    half_dim = grads_in.shape[-1] // 2
    moved = grads_in * sines
    return grads_in * cosines + jnp.concatenate(
        [moved[..., half_dim:], -moved[..., :half_dim]], axis=-1
    )


def rms_scale(values):
    return lax.rsqrt(jnp.mean(values * values, axis=-1, keepdims=True) + EPSILON)


def product(left, right):
    return jnp.dot(left, right, preferred_element_type=jnp.float32)


def contract_rows(left, right):
    return lax.dot_general(
        left, right, (((0,), (0,)), ((), ())), preferred_element_type=jnp.float32
    )


def contract_cols(left, right):
    return lax.dot_general(
        left, right, (((1,), (1,)), ((), ())), preferred_element_type=jnp.float32
    )


def rounded_wide(values):
    return lax.optimization_barrier(values.astype(jnp.bfloat16)).astype(jnp.float32)


def assemble(stacked, row_parts, col_parts):
    height, width = (stacked.shape[1], stacked.shape[2])
    grid = stacked.reshape(row_parts, col_parts, height, width).transpose(0, 2, 1, 3)
    return grid.reshape(row_parts * height, col_parts * width)


def split_blocks(full, row_parts, col_parts):
    height = full.shape[0] // row_parts
    width = full.shape[1] // col_parts
    grid = full.reshape(row_parts, height, col_parts, width).transpose(0, 2, 1, 3)
    return grid.reshape(row_parts * col_parts, height, width)


def unpack_attention(stacked, row_parts, col_parts):
    matrices = tuple((assemble(member, row_parts, col_parts) for member in stacked[:4]))
    return matrices + tuple(stacked[4:])


def masked_scores(query_heads, keys_window, visible, score_scale):
    scores = jnp.einsum(
        "tkgd,skd->kgts", query_heads, keys_window, preferred_element_type=jnp.float32
    )
    return jnp.where(visible, scores * score_scale, -jnp.inf)


def shards(
    hidden_in,
    out_grad,
    seq_lengths,
    norm1_gain,
    q_weight,
    q_bias,
    k_weight,
    k_bias,
    v_weight,
    v_bias,
    o_weight,
    norm2_gain,
    gate_weight,
    up_weight,
    down_weight,
):
    row_parts = lax.axis_size("row")
    col_parts = lax.axis_size("col")
    col_place = lax.axis_index("col")
    stacked = (
        lax.all_gather(q_weight[None], ("row", "col"), axis=0, tiled=True),
        lax.all_gather(k_weight[None], ("row", "col"), axis=0, tiled=True),
        lax.all_gather(v_weight[None], ("row", "col"), axis=0, tiled=True),
        lax.all_gather(o_weight[None], ("row", "col"), axis=0, tiled=True),
        lax.all_gather(q_bias, ("row", "col"), axis=0, tiled=True),
        lax.all_gather(k_bias, ("row", "col"), axis=0, tiled=True),
        lax.all_gather(v_bias, ("row", "col"), axis=0, tiled=True),
        lax.all_gather(norm1_gain, ("row", "col"), axis=0, tiled=True),
        lax.all_gather(norm2_gain, ("row", "col"), axis=0, tiled=True),
    )
    attention = unpack_attention(stacked, row_parts, col_parts)
    gate_block, up_block, down_block = (
        lax.all_gather(gate_weight, "row", axis=0, tiled=True),
        lax.all_gather(up_weight, "row", axis=0, tiled=True),
        lax.all_gather(down_weight, "row", axis=1, tiled=True),
    )
    (
        query_matrix,
        key_matrix,
        value_matrix,
        output_matrix,
        query_offset,
        key_offset,
        value_offset,
        first_gain,
        second_gain,
    ) = attention
    own_rows = hidden_in.shape[0]
    row_tokens = own_rows * col_parts
    lengths = seq_lengths[0]
    query_slots = col_place * own_rows + jnp.arange(own_rows, dtype=jnp.int32)
    query_starts = seq_starts(query_slots, lengths)
    cosines, sines = rope_tables(query_slots - query_starts, HD)
    group_size = HQ // KVH
    score_scale = 1.0 / math.sqrt(HD)
    inputs_wide = hidden_in.astype(jnp.float32)
    first_rms = rms_scale(inputs_wide)
    first_unit = inputs_wide * first_rms
    first_normed = (first_unit * first_gain.astype(jnp.float32)).astype(jnp.bfloat16)
    query_base = product(first_normed, query_matrix) + query_offset.astype(jnp.float32)
    key_base = product(first_normed, key_matrix) + key_offset.astype(jnp.float32)
    value_own = (product(first_normed, value_matrix) + value_offset.astype(jnp.float32)).astype(
        jnp.bfloat16
    )
    queries = rotate_pairs(query_base.reshape(own_rows, HQ, HD), cosines, sines).astype(
        jnp.bfloat16
    )
    keys_own = rotate_pairs(key_base.reshape(own_rows, KVH, HD), cosines, sines).astype(
        jnp.bfloat16
    )
    keys_all, values_all = (
        lax.all_gather(keys_own.reshape(own_rows, KVH * HD), "col", axis=0, tiled=True),
        lax.all_gather(value_own, "col", axis=0, tiled=True),
    )
    window = min(own_rows + MAXLEN, row_tokens)
    window_start = jnp.clip(col_place * own_rows - MAXLEN, 0, row_tokens - window)
    key_slots = window_start + jnp.arange(window, dtype=jnp.int32)
    key_starts = seq_starts(key_slots, lengths)
    visible = (query_starts[:, None] == key_starts[None, :]) & (
        key_slots[None, :] <= query_slots[:, None]
    )
    keys_window = lax.dynamic_slice_in_dim(keys_all, window_start, window, 0).reshape(
        window, KVH, HD
    )
    values_window = lax.dynamic_slice_in_dim(values_all, window_start, window, 0).reshape(
        window, KVH, HD
    )
    query_heads = queries.reshape(own_rows, KVH, group_size, HD)
    scores = masked_scores(query_heads, keys_window, visible, score_scale)
    peak = jnp.max(scores, axis=-1, keepdims=True)
    expanded = jnp.exp(scores - peak)
    totals = jnp.sum(expanded, axis=-1, keepdims=True)
    probs = expanded / totals
    log_total = peak + jnp.log(totals)
    mixed = jnp.einsum(
        "kgts,skd->tkgd",
        probs.astype(jnp.bfloat16),
        values_window,
        preferred_element_type=jnp.float32,
    )
    mixed = mixed.reshape(own_rows, HQ * HD).astype(jnp.bfloat16)
    residual = inputs_wide + product(mixed, output_matrix)
    second_rms = rms_scale(residual)
    second_unit = residual * second_rms
    second_normed = (second_unit * second_gain.astype(jnp.float32)).astype(jnp.bfloat16)
    normed_rows = lax.all_gather(second_normed, "col", axis=0, tiled=True)
    gate_act = product(normed_rows, gate_block)
    up_act = product(normed_rows, up_block)
    sigmoid_gate = jax.nn.sigmoid(gate_act)
    silu_gate = gate_act * sigmoid_gate
    hidden = (silu_gate * up_act).astype(jnp.bfloat16)
    branch_out = lax.psum_scatter(
        product(hidden, down_block), "col", scatter_dimension=0, tiled=True
    )
    layer_out = residual + branch_out
    stacked_again = (
        lax.all_gather(q_weight[None], ("row", "col"), axis=0, tiled=True),
        lax.all_gather(k_weight[None], ("row", "col"), axis=0, tiled=True),
        lax.all_gather(v_weight[None], ("row", "col"), axis=0, tiled=True),
        lax.all_gather(o_weight[None], ("row", "col"), axis=0, tiled=True),
        lax.all_gather(q_bias, ("row", "col"), axis=0, tiled=True),
        lax.all_gather(k_bias, ("row", "col"), axis=0, tiled=True),
        lax.all_gather(v_bias, ("row", "col"), axis=0, tiled=True),
        lax.all_gather(norm1_gain, ("row", "col"), axis=0, tiled=True),
        lax.all_gather(norm2_gain, ("row", "col"), axis=0, tiled=True),
    )
    (
        query_matrix,
        key_matrix,
        value_matrix,
        output_matrix,
        query_offset,
        key_offset,
        value_offset,
        first_gain,
        second_gain,
    ) = unpack_attention(stacked_again, row_parts, col_parts)
    gate_block, up_block, down_block = (
        lax.all_gather(gate_weight, "row", axis=0, tiled=True),
        lax.all_gather(up_weight, "row", axis=0, tiled=True),
        lax.all_gather(down_weight, "row", axis=1, tiled=True),
    )
    out_rows = lax.all_gather(out_grad, "col", axis=0, tiled=True)
    hidden_grad = contract_cols(out_rows, down_block)
    down_grad = contract_rows(hidden, out_rows)
    up_grad_act = (hidden_grad * silu_gate).astype(jnp.bfloat16)
    gate_grad_act = (
        hidden_grad * up_act * sigmoid_gate * (1.0 + gate_act * (1.0 - sigmoid_gate))
    ).astype(jnp.bfloat16)
    gate_grad = contract_rows(normed_rows, gate_grad_act)
    up_grad = contract_rows(normed_rows, up_grad_act)
    normed_grad = lax.psum_scatter(
        contract_cols(gate_grad_act, gate_block) + contract_cols(up_grad_act, up_block),
        "col",
        scatter_dimension=0,
        tiled=True,
    )
    second_gain_grad = jnp.sum(normed_grad * second_unit, axis=0)
    unit_grad = normed_grad * second_gain.astype(jnp.float32)
    residual_grad = out_grad.astype(jnp.float32) + second_rms * (
        unit_grad - second_unit * jnp.mean(unit_grad * second_unit, axis=-1, keepdims=True)
    )
    attended_grad = residual_grad.astype(jnp.bfloat16)
    mixed_grad = contract_cols(attended_grad, output_matrix).astype(jnp.bfloat16)
    grad_heads = mixed_grad.reshape(own_rows, KVH, group_size, HD)
    scores = masked_scores(query_heads, keys_window, visible, score_scale)
    probs = jnp.exp(scores - log_total)
    prob_grad = jnp.einsum(
        "tkgd,skd->kgts", grad_heads, values_window, preferred_element_type=jnp.float32
    )
    value_part = jnp.einsum(
        "kgts,tkgd->skd", probs.astype(jnp.bfloat16), grad_heads, preferred_element_type=jnp.float32
    )
    score_grad = (probs * (prob_grad - jnp.sum(probs * prob_grad, axis=-1, keepdims=True))).astype(
        jnp.bfloat16
    )
    query_grad = (
        jnp.einsum("kgts,skd->tkgd", score_grad, keys_window, preferred_element_type=jnp.float32)
        * score_scale
    )
    key_part = (
        jnp.einsum("kgts,tkgd->skd", score_grad, query_heads, preferred_element_type=jnp.float32)
        * score_scale
    )
    empty_rows = jnp.zeros((row_tokens, KVH * HD), jnp.float32)
    key_rows = lax.dynamic_update_slice_in_dim(
        empty_rows, key_part.reshape(window, KVH * HD), window_start, 0
    )
    value_rows = lax.dynamic_update_slice_in_dim(
        empty_rows, value_part.reshape(window, KVH * HD), window_start, 0
    )
    key_grad, value_grad = (
        lax.psum_scatter(key_rows, "col", scatter_dimension=0, tiled=True),
        lax.psum_scatter(value_rows, "col", scatter_dimension=0, tiled=True),
    )
    query_wide = rounded_wide(query_grad.reshape(own_rows, HQ, HD))
    query_base_grad = (
        rotate_back(query_wide, cosines, sines).reshape(own_rows, HQ * HD).astype(jnp.bfloat16)
    )
    key_wide = rounded_wide(key_grad.reshape(own_rows, KVH, HD))
    key_base_grad = (
        rotate_back(key_wide, cosines, sines).reshape(own_rows, KVH * HD).astype(jnp.bfloat16)
    )
    value_base_grad = value_grad.astype(jnp.bfloat16)
    query_b_grad = jnp.sum(query_base_grad.astype(jnp.float32), axis=0)
    key_b_grad = jnp.sum(key_base_grad.astype(jnp.float32), axis=0)
    value_b_grad = jnp.sum(value_base_grad.astype(jnp.float32), axis=0)
    first_normed_grad = (
        contract_cols(query_base_grad, query_matrix)
        + contract_cols(key_base_grad, key_matrix)
        + contract_cols(value_base_grad, value_matrix)
    )
    first_gain_grad = jnp.sum(first_normed_grad * first_unit, axis=0)
    first_unit_grad = first_normed_grad * first_gain.astype(jnp.float32)
    input_grad = residual_grad + first_rms * (
        first_unit_grad
        - first_unit * jnp.mean(first_unit_grad * first_unit, axis=-1, keepdims=True)
    )
    attn_grads = (
        lax.psum_scatter(
            split_blocks(contract_rows(first_normed, query_base_grad), row_parts, col_parts),
            ("row", "col"),
            scatter_dimension=0,
            tiled=True,
        ),
        lax.psum_scatter(
            split_blocks(contract_rows(first_normed, key_base_grad), row_parts, col_parts),
            ("row", "col"),
            scatter_dimension=0,
            tiled=True,
        ),
        lax.psum_scatter(
            split_blocks(contract_rows(first_normed, value_base_grad), row_parts, col_parts),
            ("row", "col"),
            scatter_dimension=0,
            tiled=True,
        ),
        lax.psum_scatter(
            split_blocks(contract_rows(mixed, attended_grad), row_parts, col_parts),
            ("row", "col"),
            scatter_dimension=0,
            tiled=True,
        ),
        lax.psum_scatter(query_b_grad, ("row", "col"), scatter_dimension=0, tiled=True),
        lax.psum_scatter(key_b_grad, ("row", "col"), scatter_dimension=0, tiled=True),
        lax.psum_scatter(value_b_grad, ("row", "col"), scatter_dimension=0, tiled=True),
        lax.psum_scatter(first_gain_grad, ("row", "col"), scatter_dimension=0, tiled=True),
        lax.psum_scatter(second_gain_grad, ("row", "col"), scatter_dimension=0, tiled=True),
    )
    query_w_out = attn_grads[0][0]
    key_w_out = attn_grads[1][0]
    value_w_out = attn_grads[2][0]
    output_w_out = attn_grads[3][0]
    small_out = attn_grads[4:9]
    mlp_grads = (
        lax.psum_scatter(gate_grad, "row", scatter_dimension=0, tiled=True),
        lax.psum_scatter(up_grad, "row", scatter_dimension=0, tiled=True),
        lax.psum_scatter(down_grad, "row", scatter_dimension=1, tiled=True),
    )
    return (
        layer_out,
        input_grad,
        small_out[3],
        query_w_out,
        small_out[0],
        key_w_out,
        small_out[1],
        value_w_out,
        small_out[2],
        output_w_out,
        small_out[4],
        mlp_grads[0],
        mlp_grads[1],
        mlp_grads[2],
    )


def solution(mesh):
    in_specs = (
        P(("row", "col"), None),
        P(("row", "col"), None),
        P("row", None),
        P(("row", "col")),
        P("row", "col"),
        P(("row", "col")),
        P("row", "col"),
        P(("row", "col")),
        P("row", "col"),
        P(("row", "col")),
        P("row", "col"),
        P(("row", "col")),
        P("row", "col"),
        P("row", "col"),
        P("col", "row"),
    )
    out_specs = (
        P(("row", "col"), None),
        P(("row", "col"), None),
        P(("row", "col")),
        P("row", "col"),
        P(("row", "col")),
        P("row", "col"),
        P(("row", "col")),
        P("row", "col"),
        P(("row", "col")),
        P("row", "col"),
        P(("row", "col")),
        P("row", "col"),
        P("row", "col"),
        P("col", "row"),
    )
    return jax.shard_map(shards, mesh=mesh, in_specs=in_specs, out_specs=out_specs, check_vma=False)
```

profile of v0, /device:TPU:0, one launch (start us, length us, event | category | flops | bytes accessed | tf_op | source)
XLA Modules:
  0.0 1829.9 jit_solution(13234642449965689146)
XLA Ops:
  11.6 42.2 %all-reduce.11 = (bf16[256]{0:T(256)(128)(2,1)S(1)}, bf16[1536]{0:T(1024)(128)(2,1)S(1)}, bf16[256]{0:T(256)(128)(2,1)S(1)}, bf16[1536]{0:T(1024)(128)(2,1)S(1)}, bf16[1536]{0:T(1024)(128)(2,1)S(1)}) all-reduce(bf16[256]{0:T(256)(128)(2,1)S(1)} %dynamic-update-slice.1, ...), channel_id=1, replica_groups=mesh['row'=4,'col'=8] {'row','col'}, use_global_device_ids=true, to_apply=%add.1 | all-reduce | flops 5120 | bytes 20480
  55.2 42.7 %all-gather = bf16[12288,32]{0,1:T(8,128)(2,1)S(1)} all-gather(bf16[384,32]{0,1:T(8,128)(2,1)} %param.23), channel_id=2, replica_groups=mesh['row'=4,'col'=8] {'row','col'}, dimensions={0}, use_global_device_ids=true | all-gather | bytes 811008 | tf_op jit(solution)/shard_map/all_gather | solution.py:115
  100.5 39.0 %all-gather.1 = bf16[12288,32]{0,1:T(8,128)(2,1)S(1)} all-gather(bf16[384,32]{0,1:T(8,128)(2,1)S(1)} %copy-done.32), channel_id=3, replica_groups=mesh['row'=4,'col'=8] {'row','col'}, dimensions={0}, use_global_device_ids=true | all-gather | bytes 811008 | tf_op jit(solution)/shard_map/all_gather | solution.py:114
  148.0 15.2 all-gather.16.cloned.1.call-done
  164.7 65.0 %all-gather.28.cloned.1.call-done = bf16[12288,192]{0,1:T(8,128)(2,1)} async-done(((bf16[384,192]{0,1:T(8,128)(2,1)}), bf16[12288,192]{0,1:T(8,128)(2,1)}) %all-gather.28.cloned.1.call-update) | async-done | bytes 4718608 | tf_op jit(solution)/shard_map/all_gather | solution.py:113
  229.6 3.3 copy.161
  233.0 1.8 copy.115
  235.7 2.1 copy-done.10
  237.8 2.6 convolution_add_fusion.4
  240.4 1.9 copy.116
  243.6 50.6 %all-gather.30.cloned.1.call-done = bf16[12288,192]{0,1:T(8,128)(2,1)} async-done(((bf16[384,192]{0,1:T(8,128)(2,1)}), bf16[12288,192]{0,1:T(8,128)(2,1)}) %all-gather.30.cloned.1.call-update) | async-done | bytes 4718608 | tf_op jit(solution)/shard_map/all_gather | solution.py:116
  294.2 3.3 copy.163
  297.5 1.8 copy.121
  301.3 16.6 fusion.46
  317.9 7.7 fusion.3
  325.6 7.3 fusion.26
  332.9 1.5 multiply_reduce_fusion.2
  337.8 24.1 %all-gather.20.cloned.1.call-done = bf16[1536,1120]{0,1:T(8,128)(2,1)} async-done(((bf16[384,1120]{0,1:T(8,128)(2,1)}), bf16[1536,1120]{0,1:T(8,128)(2,1)}) %all-gather.20.cloned.1.call-update) | async-done | bytes 3440656 | tf_op jit(solution)/shard_map/all_gather | solution.py:125
  361.9 46.3 %all-gather.18.cloned.1.call-done = bf16[2048,1536]{1,0:T(8,128)(2,1)} async-done(((bf16[256,1536]{1,0:T(8,128)(2,1)}), bf16[2048,1536]{1,0:T(8,128)(2,1)}) %all-gather.18.cloned.1.call-update) | async-done | bytes 6291472 | tf_op jit(solution)/shard_map/all_gather | solution.py:198
  408.2 12.9 fusion.47
  421.1 56.8 %all-gather.22.cloned.1.call-done = bf16[1536,1120]{0,1:T(8,128)(2,1)} async-done(((bf16[384,1120]{0,1:T(8,128)(2,1)}), bf16[1536,1120]{0,1:T(8,128)(2,1)}) %all-gather.22.cloned.1.call-update) | async-done | bytes 3440656 | tf_op jit(solution)/shard_map/all_gather | solution.py:126
  477.9 12.9 fusion.48
  490.8 55.4 %all-gather.24.cloned.1.call-done = bf16[1120,1536]{1,0:T(8,128)(2,1)} async-done(((bf16[1120,384]{1,0:T(8,128)(2,1)}), bf16[1120,1536]{1,0:T(8,128)(2,1)}) %all-gather.24.cloned.1.call-update) | async-done | bytes 3440656 | tf_op jit(solution)/shard_map/all_gather | solution.py:127
  546.2 45.9 %all-gather.26.cloned.1.call-done = bf16[2048,1536]{1,0:T(8,128)(2,1)} async-done(((bf16[256,1536]{1,0:T(8,128)(2,1)}), bf16[2048,1536]{1,0:T(8,128)(2,1)}) %all-gather.26.cloned.1.call-update) | async-done | bytes 6291472 | tf_op jit(solution)/shard_map/all_gather | solution.py:235
  592.1 20.8 %multiply_convert_fusion = (bf16[2048,1120]{0,1:T(8,128)(2,1)}, bf16[2048,1120]{0,1:T(8,128)(2,1)}, bf16[2048,1120]{0,1:T(8,128)(2,1)}) fusion(f32[2048,1120]{0,1:T(8,128)} %fusion.47, f32[2048,1120]{0,1:T(8,128)} %fusion.48, bf16[2048,1536]{1,0:T(8,128)(2,1)} %all-gather.26.cloned.1.call-done, bf16[1120,1536]{1,0:T(8,128)(2,1)} %all-gather.24.cloned.1.call-done), kind=kOutput, calls=%fused_computation.11 | convolution fusion | flops 7080837120 | bytes 41844736 | tf_op jit(solution)/shard_map/dot_general | solution.py:58
  612.9 13.4 fusion.50
  626.3 14.0 convolution_add_fusion
  640.4 15.2 fusion.49
  655.9 76.9 %reduce-scatter.14.cloned.1.call-done = f32[256,1536]{1,0:T(8,128)} async-done(((f32[2048,1536]{1,0:T(8,128)}), f32[256,1536]{1,0:T(8,128)}) %reduce-scatter.14.cloned.1.call-update) | async-done | bytes 1572880 | tf_op jit(solution)/shard_map/reduce_scatter | solution.py:244
  732.8 1.9 multiply_reduce_fusion
  734.6 94.0 %reduce-scatter.12.cloned.1.call-done = f32[256,1536]{1,0:T(8,128)} async-done(((f32[2048,1536]{1,0:T(8,128)}), f32[256,1536]{1,0:T(8,128)}) %reduce-scatter.12.cloned.1.call-update) | async-done | bytes 1572880 | tf_op jit(solution)/shard_map/reduce_scatter | solution.py:204
  828.6 3.8 convert_bitcast_fusion
  833.5 3.7 convolution_convert_fusion
  837.6 12.6 fusion
  850.3 1.9 slice-done.2
  853.1 7.5 fusion.2
  860.6 3.7 fusion.10
  864.5 9.9 dynamic_update_slice.6
  875.8 7.0 fusion.6
  883.0 10.8 dynamic_update_slice.7
  895.3 12.9 fusion.56
  908.4 12.8 fusion.57
  921.3 12.6 fusion.55
  935.0 4.4 multiply_convert_fusion.3
  942.2 5.0 fusion.51
  948.9 3.0 convolution_add_fusion.2
  952.0 9.5 reduce-scatter.18.cloned.1.call-done
  961.5 1.9 convolution_add_fusion.1
  967.2 1.5 fusion.53
  968.8 2.3 fusion.34
  971.2 3.0 reshape.290
  974.1 2.8 copy.131
  977.2 2.3 copy.132
  979.5 6.4 fusion.54
  986.1 6.2 fusion.52
  993.0 44.7 %all-reduce.10 = (f32[1536]{0:T(1024)S(1)}, f32[1536]{0:T(1024)S(1)}, f32[256]{0:T(256)S(1)}, f32[256]{0:T(256)S(1)}, f32[1536]{0:T(1024)S(1)}) all-reduce(f32[1536]{0:T(1024)S(1)} %copy-done.31, f32[1536]{0:T(1024)S(1)} %bitcast.257, f32[256]{0:T(256)S(1)} %bitcast.261, ...), channel_id=10, replica_groups=mesh['row'=4,'col'=8] {'row','col'}, use_global_device_ids=true, to_apply=%region_15.16.clone | all-reduce | flops 5120 | bytes 40960
  1040.6 3.0 fusion.21
  1043.5 42.1 %reduce-scatter.28.cloned.1.call-done = f32[384,1120]{0,1:T(8,128)} async-done(((f32[1536,1120]{0,1:T(8,128)}), f32[384,1120]{0,1:T(8,128)}) %reduce-scatter.28.cloned.1.call-update) | async-done | bytes 1720336 | tf_op jit(solution)/shard_map/reduce_scatter | solution.py:348
  1085.6 123.6 %reduce-scatter.30.cloned.1.call-done = f32[384,1120]{0,1:T(8,128)} async-done(((f32[1536,1120]{0,1:T(8,128)}), f32[384,1120]{0,1:T(8,128)}) %reduce-scatter.30.cloned.1.call-update) | async-done | bytes 1720336 | tf_op jit(solution)/shard_map/reduce_scatter | solution.py:349
  1209.2 123.6 %reduce-scatter.32.cloned.1.call-done = f32[1120,384]{1,0:T(8,128)} async-done(((f32[1120,1536]{1,0:T(8,128)}), f32[1120,384]{1,0:T(8,128)}) %reduce-scatter.32.cloned.1.call-update) | async-done | bytes 1720336 | tf_op jit(solution)/shard_map/reduce_scatter | solution.py:350
  1332.8 104.1 %reduce-scatter.22.cloned.1.call-done = f32[1,384,32]{1,2,0:T(8,128)} async-done(((f32[32,384,32]{1,2,0:T(8,128)}), f32[1,384,32]{1,2,0:T(8,128)}) %reduce-scatter.22.cloned.1.call-update) | async-done | bytes 49168 | tf_op jit(solution)/shard_map/reduce_scatter | solution.py:318
  1437.0 102.6 %reduce-scatter.24.cloned.1.call-done = f32[1,384,32]{1,2,0:T(8,128)} async-done(((f32[32,384,32]{1,2,0:T(8,128)}), f32[1,384,32]{1,2,0:T(8,128)}) %reduce-scatter.24.cloned.1.call-update) | async-done | bytes 49168 | tf_op jit(solution)/shard_map/reduce_scatter | solution.py:324
  1539.6 141.7 %reduce-scatter.26.cloned.1.call-done = f32[1,384,192]{1,2,0:T(8,128)} async-done(((f32[32,384,192]{1,2,0:T(8,128)}), f32[1,384,192]{1,2,0:T(8,128)}) %reduce-scatter.26.cloned.1.call-update) | async-done | bytes 294928 | tf_op jit(solution)/shard_map/reduce_scatter | solution.py:330
  1681.3 141.5 %reduce-scatter.20.cloned.1.call-done = f32[1,384,192]{1,2,0:T(8,128)} async-done(((f32[32,384,192]{1,2,0:T(8,128)}), f32[1,384,192]{1,2,0:T(8,128)}) %reduce-scatter.20.cloned.1.call-update) | async-done | bytes 294928 | tf_op jit(solution)/shard_map/reduce_scatter | solution.py:312
  (204 shorter events, 45.0 us)
Async XLA Ops:
  7.2 92.2 %copy-start.1 = (bf16[256,1536]{1,0:T(8,128)(2,1)S(1)}, bf16[256,1536]{1,0:T(8,128)(2,1)}, u32[]{:S(2)}) copy-start(bf16[256,1536]{1,0:T(8,128)(2,1)} %param.15) | copy-start | bytes 2359300
  7.2 138.5 %all-gather.14.cloned.1.call-start = ((), (), s32[]{:S(2)}) async-start(), calls=%async_computation.11 | async-start | bytes 1179648 | tf_op jit(solution)/shard_map/all_gather | solution.py:165
  53.8 181.9 %copy-start.28 = (f32[1536]{0:T(1024)}, f32[1536]{0:T(1024)S(1)}, u32[]{:S(2)}) copy-start(f32[1536]{0:T(1024)S(1)} %convert_element_type.134) | copy-start | bytes 18436
  55.2 180.6 %copy-start.33 = (f32[256]{0:T(256)}, f32[256]{0:T(256)S(1)}, u32[]{:S(2)}) copy-start(f32[256]{0:T(256)S(1)} %add_rsqrt_fusion.1) | copy-start | bytes 3076
  97.9 2.6 copy-start.32
  98.4 0.9 copy-start.18
  100.4 39.6 %copy-start.36 = (s32[1,16]{1,0:T(1,128)S(1)}, s32[1,16]{1,0:T(1,128)}, u32[]{:S(2)}) copy-start(s32[1,16]{1,0:T(1,128)} %param.17) | copy-start | bytes 196
  100.5 62.8 %all-gather.16.cloned.1.call-start = ((), (), s32[]{:S(2)}) async-start(), calls=%async_computation.12 | async-start | bytes 1179648 | tf_op jit(solution)/shard_map/all_gather | solution.py:164
  140.0 4.6 copy-start.22
  141.0 3.7 copy-start.14
  141.0 159.3 %copy-start.12 = (f32[256,128]{0,1:T(8,128)}, f32[256,128]{0,1:T(8,128)S(1)}, u32[]{:S(2)}) copy-start(f32[256,128]{0,1:T(8,128)S(1)} %get-tuple-element.47) | copy-start | bytes 393220
  142.3 87.4 %all-gather.28.cloned.1.call-start = ((), (), s32[]{:S(2)}) async-start(), calls=%async_computation.29 | async-start | bytes 4866048 | tf_op jit(solution)/shard_map/all_gather | solution.py:113
  143.0 151.2 %all-gather.30.cloned.1.call-start = ((), (), s32[]{:S(2)}) async-start(), calls=%async_computation.30 | async-start | bytes 4866048 | tf_op jit(solution)/shard_map/all_gather | solution.py:116
  143.6 218.3 %all-gather.20.cloned.1.call-start = ((), (), s32[]{:S(2)}) async-start(), calls=%async_computation.14 | async-start | bytes 4300800 | tf_op jit(solution)/shard_map/all_gather | solution.py:125
  144.2 264.0 %all-gather.18.cloned.1.call-start = ((), (), s32[]{:S(2)}) async-start(), calls=%async_computation.13 | async-start | bytes 7077888 | tf_op jit(solution)/shard_map/all_gather | solution.py:198
  164.6 136.6 %copy-start.8 = (bf16[1280,256]{0,1:T(8,128)(2,1)}, bf16[1280,256]{0,1:T(8,128)(2,1)S(1)}, u32[]{:S(2)}) copy-start(bf16[1280,256]{0,1:T(8,128)(2,1)S(1)} %constant_dynamic-slice_fusion) | copy-start | bytes 1966084
  235.7 2.1 copy-start.10
  299.4 0.9 copy-start.15
  299.4 1.3 copy-start.20
  299.4 1.6 copy-start.21
  300.2 32.6 %copy-start.11 = (bf16[192,8,4,384]{3,1,2,0:T(8,128)(2,1)}, bf16[192,8,4,384]{3,1,2,0:T(8,128)(2,1)S(1)}, u32[]{:S(2)}) copy-start(bf16[192,8,4,384]{3,1,2,0:T(8,128)(2,1)S(1)} %copy.164) | copy-start | bytes 14155780
  301.2 16.6 copy-start.3
  317.9 7.7 copy-start.25
  332.8 1.6 copy-start.27
  335.5 142.4 %all-gather.22.cloned.1.call-start = ((), (), s32[]{:S(2)}) async-start(), calls=%async_computation.15 | async-start | bytes 4300800 | tf_op jit(solution)/shard_map/all_gather | solution.py:126
  336.3 209.9 %all-gather.24.cloned.1.call-start = ((), (), s32[]{:S(2)}) async-start(), calls=%async_computation.16 | async-start | bytes 4300800 | tf_op jit(solution)/shard_map/all_gather | solution.py:127
  337.0 255.0 %all-gather.26.cloned.1.call-start = ((), (), s32[]{:S(2)}) async-start(), calls=%async_computation.18 | async-start | bytes 7077888 | tf_op jit(solution)/shard_map/all_gather | solution.py:235
  337.8 395.0 %reduce-scatter.14.cloned.1.call-start = ((), (), s32[]{:S(2)}) async-start(), calls=%async_computation.19 | async-start | bytes 14155776 | tf_op jit(solution)/shard_map/reduce_scatter | solution.py:244
  592.1 20.8 %copy-start.39 = (bf16[1536,1120]{0,1:T(8,128)(2,1)S(1)}, bf16[1536,1120]{0,1:T(8,128)(2,1)}, u32[]{:S(2)}) copy-start(bf16[1536,1120]{0,1:T(8,128)(2,1)} %all-gather.20.cloned.1.call-done) | copy-start | bytes 10321924
  612.8 13.5 copy-start.40
  612.9 13.5 copy-start.41
  640.3 188.3 %reduce-scatter.12.cloned.1.call-start = ((), (), s32[]{:S(2)}) async-start(), calls=%async_computation.17 | async-start | bytes 14155776 | tf_op jit(solution)/shard_map/reduce_scatter | solution.py:204
  655.6 173.0 %copy-start.17 = (bf16[256,1536]{1,0:T(8,128)(2,1)S(1)}, bf16[256,1536]{1,0:T(8,128)(2,1)}, u32[]{:S(2)}) copy-start(bf16[256,1536]{1,0:T(8,128)(2,1)} %param.16) | copy-start | bytes 2359300
  655.6 291.5 %reduce-scatter.16.cloned.1.call-start = ((), (), s32[]{:S(2)}) async-start(), calls=%async_computation.20 | async-start | bytes 2359296 | tf_op jit(solution)/shard_map/reduce_scatter | solution.py:285
  832.4 1.1 copy-start.7
  837.6 12.7 slice-start
  837.6 12.7 slice-start.1
  837.6 14.6 slice-start.2
  837.6 15.5 slice-start.3
  853.1 7.5 copy-start.4
  860.6 3.7 copy-start
  874.4 1.3 copy-start.6
  875.8 85.7 %reduce-scatter.18.cloned.1.call-start = ((), (), s32[]{:S(2)}) async-start(), calls=%async_computation.21 | async-start | bytes 2359296 | tf_op jit(solution)/shard_map/reduce_scatter | solution.py:286
  893.8 1.3 copy-start.5
  895.2 190.4 %reduce-scatter.28.cloned.1.call-start = ((), (), s32[]{:S(2)}) async-start(), calls=%async_computation.26 | async-start | bytes 8601600 | tf_op jit(solution)/shard_map/reduce_scatter | solution.py:348
  908.2 301.0 %reduce-scatter.30.cloned.1.call-start = ((), (), s32[]{:S(2)}) async-start(), calls=%async_computation.27 | async-start | bytes 8601600 | tf_op jit(solution)/shard_map/reduce_scatter | solution.py:349
  921.2 411.6 %reduce-scatter.32.cloned.1.call-start = ((), (), s32[]{:S(2)}) async-start(), calls=%async_computation.28 | async-start | bytes 8601600 | tf_op jit(solution)/shard_map/reduce_scatter | solution.py:350
  933.9 1.1 copy-start.9
  933.9 5.5 copy-start.16
  933.9 503.1 %reduce-scatter.22.cloned.1.call-start = ((), (), s32[]{:S(2)}) async-start(), calls=%async_computation.23 | async-start | bytes 1622016 | tf_op jit(solution)/shard_map/reduce_scatter | solution.py:318
  939.4 0.9 copy-start.13
  941.2 0.9 copy-start.24
  942.2 6.8 copy-start.23
  947.1 14.3 copy-start.19
  948.9 14.4 copy-start.2
  948.9 14.4 copy-start.29
  948.9 14.4 copy-start.34
  964.6 4.2 copy-start.26
  968.8 570.8 %reduce-scatter.24.cloned.1.call-start = ((), (), s32[]{:S(2)}) async-start(), calls=%async_computation.24 | async-start | bytes 1622016 | tf_op jit(solution)/shard_map/reduce_scatter | solution.py:324
  976.9 704.4 %reduce-scatter.26.cloned.1.call-start = ((), (), s32[]{:S(2)}) async-start(), calls=%async_computation.25 | async-start | bytes 9732096 | tf_op jit(solution)/shard_map/reduce_scatter | solution.py:330
  986.0 836.8 %reduce-scatter.20.cloned.1.call-start = ((), (), s32[]{:S(2)}) async-start(), calls=%async_computation.22 | async-start | bytes 9732096 | tf_op jit(solution)/shard_map/reduce_scatter | solution.py:312
  992.2 0.7 copy-start.38
  992.3 48.3 %copy-start.37 = (f32[256]{0:T(256)S(1)}, f32[256]{0:T(256)}, u32[]{:S(2)}) copy-start(f32[256]{0:T(256)} %get-tuple-element.17) | copy-start | bytes 3076
  992.3 48.3 %copy-start.35 = (f32[256]{0:T(256)S(1)}, f32[256]{0:T(256)}, u32[]{:S(2)}) copy-start(f32[256]{0:T(256)} %copy-done.33) | copy-start | bytes 3076
  (2 other events, 1.4 us)
Sparse Core Ops, SparseCore 0:
  100.6 21.2 all-gather.13
  142.4 20.8 all-gather.15
  166.1 63.5 all-gather.27
  232.3 61.8 all-gather.29
  295.6 66.2 all-gather.19
  364.2 43.9 all-gather.17
  409.8 68.0 all-gather.21
  479.5 66.6 all-gather.23
  548.1 43.9 all-gather.25
  640.4 92.2 reduce-scatter.13
  736.3 92.2 reduce-scatter.11
  875.9 41.1 reduce-scatter.15
  920.3 41.0 reduce-scatter.17
  964.2 121.3 reduce-scatter.27
  1088.3 120.8 reduce-scatter.29
  1212.0 120.8 reduce-scatter.31
  1338.5 98.4 reduce-scatter.21
  1442.6 96.8 reduce-scatter.23
  1546.1 135.2 reduce-scatter.25
  1687.6 135.1 reduce-scatter.19
where the time goes:
time: 1840 us; the launch traced here: 1830 us
  waiting for transfers between devices  1320 us (72%)
  matrix products  215 us (12%)
  blocking collectives  169 us (9%)
  local copies, waits for them, and re-layouts  71.5 us (4%)
  other arithmetic  34.8 us (2%)
    reduce_scatter x1, waiting for transfers between devices, shards(): lax.psum_scatter(split_blocks(contract_rows(mixed, attended_grad), row_pa...  142 us
    reduce_scatter x1, waiting for transfers between devices, shards(): lax.psum_scatter(split_blocks(contract_rows(first_normed, query_base_grad...  142 us
    reduce_scatter x1, waiting for transfers between devices, shards(): lax.psum_scatter(down_grad, 'row', scatter_dimension=1, tiled=True)  124 us
    reduce_scatter x1, waiting for transfers between devices, shards(): lax.psum_scatter(up_grad, 'row', scatter_dimension=0, tiled=True)  124 us
    reduce_scatter x1, waiting for transfers between devices, shards(): lax.psum_scatter(split_blocks(contract_rows(first_normed, key_base_grad),...  104 us
    reduce_scatter x1, waiting for transfers between devices, shards(): lax.psum_scatter(split_blocks(contract_rows(first_normed, value_base_grad...  103 us
    reduce_scatter x1, waiting for transfers between devices, shards(): lax.psum_scatter(product(hidden, down_block), 'col', scatter_dimension=0,...  94 us
    unnamed x2, blocking collectives  86.9 us
  transfers between devices with their start and end apart: 20, of which 18 were waited for; matrix products, arithmetic and copies ran while one was open for 12% of the time, Pallas kernels for 0%

commit v1 on v0

--- a/solution.py
+++ b/solution.py
@@ -3,6 +3,7 @@
 import jax.numpy as jnp
 from jax import lax
 from jax.sharding import PartitionSpec as P
+from jax.lax import axis_index, axis_size, ppermute
 
 HQ = 12
 KVH = 2
@@ -121,10 +122,25 @@
         lax.all_gather(norm2_gain, ("row", "col"), axis=0, tiled=True),
     )
     attention = unpack_attention(stacked, row_parts, col_parts)
+
+    def number_the_sites(base_x, row_axis):
+        row_out = axis_index(row_axis)
+        vec_out = axis_size(row_axis)
+        w2, carry_in, h_now = (vec_out, row_out, base_x.shape[1])
+        history = [(q, (q + 1) % w2) for q in range(w2)]
+        block_now = base_x
+        arr_next = jnp.zeros((*base_x.shape[:1], w2 * h_now, *base_x.shape[2:]), base_x.dtype)
+        for rr in range(w2):
+            t1 = (carry_in - rr) % w2
+            arr_next = lax.dynamic_update_slice_in_dim(arr_next, block_now, t1 * h_now, axis=1)
+            if rr < w2 - 1:
+                block_now = ppermute(block_now, row_axis, history)
+        return arr_next
+
     gate_block, up_block, down_block = (
         lax.all_gather(gate_weight, "row", axis=0, tiled=True),
         lax.all_gather(up_weight, "row", axis=0, tiled=True),
-        lax.all_gather(down_weight, "row", axis=1, tiled=True),
+        number_the_sites(down_weight, "row"),
     )
     (
         query_matrix,

time: 1840 us -> 1840 us (level)
    reduce_scatter x1, waiting for transfers between devices: 76.9 us -> 10.5 us  [shards(): lax.psum_scatter(contract_cols(gate_grad_act, gate_block) + contract_cols...]
    ppermute x0 -> x3, waiting for transfers between devices: none -> 62.4 us  [number_the_sites(): block_now = ppermute(block_now, row_axis, history)]
  transfers between devices with their start and end apart: 20 -> 23, of which waited for: 18 -> 21; matrix products, arithmetic and copies ran while one was open for 12% -> 11% of each run, Pallas kernels for 0% -> 0%
where the time goes in v1:
time: 1840 us; the launch traced here: 1830 us
  waiting for transfers between devices  1320 us (72%)
  matrix products  211 us (11%)
  blocking collectives  169 us (9%)
  local copies, waits for them, and re-layouts  78 us (4%)
  other arithmetic  34.7 us (2%)
    reduce_scatter x1, waiting for transfers between devices, shards(): lax.psum_scatter(split_blocks(contract_rows(mixed, attended_grad), row_pa...  142 us
    reduce_scatter x1, waiting for transfers between devices, shards(): lax.psum_scatter(split_blocks(contract_rows(first_normed, query_base_grad...  141 us
    reduce_scatter x1, waiting for transfers between devices, shards(): lax.psum_scatter(down_grad, 'row', scatter_dimension=1, tiled=True)  124 us
    reduce_scatter x1, waiting for transfers between devices, shards(): lax.psum_scatter(up_grad, 'row', scatter_dimension=0, tiled=True)  124 us
    reduce_scatter x1, waiting for transfers between devices, shards(): lax.psum_scatter(split_blocks(contract_rows(first_normed, key_base_grad),...  104 us
    reduce_scatter x1, waiting for transfers between devices, shards(): lax.psum_scatter(split_blocks(contract_rows(first_normed, value_base_grad...  103 us
    reduce_scatter x1, waiting for transfers between devices, shards(): lax.psum_scatter(product(hidden, down_block), 'col', scatter_dimension=0,...  94 us
    unnamed x2, blocking collectives  86.9 us
  transfers between devices with their start and end apart: 23, of which 21 were waited for; matrix products, arithmetic and copies ran while one was open for 11% of the time, Pallas kernels for 0%

profile of v1, /device:TPU:0, one launch (start us, length us, event | category | flops | bytes accessed | tf_op | source)
XLA Modules:
  0.0 1829.8 jit_solution(9637498584656964820)
XLA Ops:
  11.6 42.2 %all-reduce.11 = (bf16[256]{0:T(256)(128)(2,1)S(1)}, bf16[1536]{0:T(1024)(128)(2,1)S(1)}, bf16[256]{0:T(256)(128)(2,1)S(1)}, bf16[1536]{0:T(1024)(128)(2,1)S(1)}, bf16[1536]{0:T(1024)(128)(2,1)S(1)}) all-reduce(bf16[256]{0:T(256)(128)(2,1)S(1)} %dynamic-update-slice.1, ...), channel_id=1, replica_groups=mesh['row'=4,'col'=8] {'row','col'}, use_global_device_ids=true, to_apply=%add.1 | all-reduce | flops 5120 | bytes 20480
  55.2 42.7 %all-gather = bf16[12288,32]{0,1:T(8,128)(2,1)S(1)} all-gather(bf16[384,32]{0,1:T(8,128)(2,1)} %param.23), channel_id=2, replica_groups=mesh['row'=4,'col'=8] {'row','col'}, dimensions={0}, use_global_device_ids=true | all-gather | bytes 811008 | tf_op jit(solution)/shard_map/all_gather | solution.py:116
  100.5 39.0 %all-gather.1 = bf16[12288,32]{0,1:T(8,128)(2,1)S(1)} all-gather(bf16[384,32]{0,1:T(8,128)(2,1)S(1)} %copy-done.36), channel_id=3, replica_groups=mesh['row'=4,'col'=8] {'row','col'}, dimensions={0}, use_global_device_ids=true | all-gather | bytes 811008 | tf_op jit(solution)/shard_map/all_gather | solution.py:115
  148.0 15.2 all-gather.16.cloned.1.call-done
  164.6 65.0 %all-gather.28.cloned.1.call-done = bf16[12288,192]{0,1:T(8,128)(2,1)} async-done(((bf16[384,192]{0,1:T(8,128)(2,1)}), bf16[12288,192]{0,1:T(8,128)(2,1)}) %all-gather.28.cloned.1.call-update) | async-done | bytes 4718608 | tf_op jit(solution)/shard_map/all_gather | solution.py:114
  229.6 3.3 copy.161
  235.7 2.1 copy-done.10
  237.8 2.6 convolution_add_fusion.4
  240.4 1.9 copy.116
  243.6 50.6 %all-gather.30.cloned.1.call-done = bf16[12288,192]{0,1:T(8,128)(2,1)} async-done(((bf16[384,192]{0,1:T(8,128)(2,1)}), bf16[12288,192]{0,1:T(8,128)(2,1)}) %all-gather.30.cloned.1.call-update) | async-done | bytes 4718608 | tf_op jit(solution)/shard_map/all_gather | solution.py:117
  294.2 3.3 copy.163
  301.2 16.6 fusion.46
  317.8 7.7 fusion.3
  325.5 7.3 fusion.26
  337.8 24.1 %all-gather.20.cloned.1.call-done = bf16[1536,1120]{0,1:T(8,128)(2,1)} async-done(((bf16[384,1120]{0,1:T(8,128)(2,1)}), bf16[1536,1120]{0,1:T(8,128)(2,1)}) %all-gather.20.cloned.1.call-update) | async-done | bytes 3440656 | tf_op jit(solution)/shard_map/all_gather | solution.py:141
  361.9 46.3 %all-gather.18.cloned.1.call-done = bf16[2048,1536]{1,0:T(8,128)(2,1)} async-done(((bf16[256,1536]{1,0:T(8,128)(2,1)}), bf16[2048,1536]{1,0:T(8,128)(2,1)}) %all-gather.18.cloned.1.call-update) | async-done | bytes 6291472 | tf_op jit(solution)/shard_map/all_gather | solution.py:214
  408.2 13.0 fusion.47
  421.2 56.7 %all-gather.22.cloned.1.call-done = bf16[1536,1120]{0,1:T(8,128)(2,1)} async-done(((bf16[384,1120]{0,1:T(8,128)(2,1)}), bf16[1536,1120]{0,1:T(8,128)(2,1)}) %all-gather.22.cloned.1.call-update) | async-done | bytes 3440656 | tf_op jit(solution)/shard_map/all_gather | solution.py:142
  477.9 12.9 fusion.48
  490.8 55.4 %all-gather.26.cloned.1.call-done = bf16[1120,1536]{1,0:T(8,128)(2,1)} async-done(((bf16[1120,384]{1,0:T(8,128)(2,1)}), bf16[1120,1536]{1,0:T(8,128)(2,1)}) %all-gather.26.cloned.1.call-update) | async-done | bytes 3440656 | tf_op jit(solution)/shard_map/all_gather | solution.py:249
  546.2 45.9 %all-gather.24.cloned.1.call-done = bf16[2048,1536]{1,0:T(8,128)(2,1)} async-done(((bf16[256,1536]{1,0:T(8,128)(2,1)}), bf16[2048,1536]{1,0:T(8,128)(2,1)}) %all-gather.24.cloned.1.call-update) | async-done | bytes 6291472 | tf_op jit(solution)/shard_map/all_gather | solution.py:251
  592.1 20.8 %multiply_convert_fusion = (bf16[2048,1120]{0,1:T(8,128)(2,1)}, bf16[2048,1120]{0,1:T(8,128)(2,1)}, bf16[2048,1120]{0,1:T(8,128)(2,1)}) fusion(f32[2048,1120]{0,1:T(8,128)} %fusion.47, f32[2048,1120]{0,1:T(8,128)} %fusion.48, bf16[2048,1536]{1,0:T(8,128)(2,1)} %all-gather.24.cloned.1.call-done, bf16[1120,1536]{1,0:T(8,128)(2,1)} %all-gather.26.cloned.1.call-done), kind=kOutput, calls=%fused_computation.11 | convolution fusion | flops 7080837120 | bytes 41844736 | tf_op jit(solution)/shard_map/dot_general | solution.py:59
  612.9 13.4 fusion.50
  626.3 14.0 convolution_add_fusion
  642.9 21.6 %collective-permute-done = bf16[1120,384]{1,0:T(8,128)(2,1)S(1)} collective-permute-done((bf16[1120,384]{1,0:T(8,128)(2,1)S(1)}, bf16[1120,384]{1,0:T(8,128)(2,1)S(1)}, u32[]{:S(2)}, u32[]{:S(2)}) %collective-permute-start) | collective-permute-done | bytes 860192 | tf_op jit(solution)/shard_map/ppermute | solution.py:137
  665.4 22.3 %collective-permute-done.1 = bf16[1120,384]{1,0:T(8,128)(2,1)} collective-permute-done((bf16[1120,384]{1,0:T(8,128)(2,1)S(1)}, bf16[1120,384]{1,0:T(8,128)(2,1)}, u32[]{:S(2)}, u32[]{:S(2)}) %collective-permute-start.1) | collective-permute-done | bytes 860192 | tf_op jit(solution)/shard_map/ppermute | solution.py:137
  689.1 1.9 constant_dynamic-update-slice_fusion.1
  691.0 18.4 %collective-permute-done.2 = bf16[1120,384]{1,0:T(8,128)(2,1)} collective-permute-done((bf16[1120,384]{1,0:T(8,128)(2,1)}, bf16[1120,384]{1,0:T(8,128)(2,1)}, u32[]{:S(2)}, u32[]{:S(2)}) %collective-permute-start.2) | collective-permute-done | bytes 860192 | tf_op jit(solution)/shard_map/ppermute | solution.py:137
  710.8 11.2 fusion.49
  722.3 10.5 reduce-scatter.14.cloned.1.call-done
  732.7 1.9 multiply_reduce_fusion
  734.6 94.0 %reduce-scatter.12.cloned.1.call-done = f32[256,1536]{1,0:T(8,128)} async-done(((f32[2048,1536]{1,0:T(8,128)}), f32[256,1536]{1,0:T(8,128)}) %reduce-scatter.12.cloned.1.call-update) | async-done | bytes 1572880 | tf_op jit(solution)/shard_map/reduce_scatter | solution.py:220
  828.6 3.8 convert_bitcast_fusion
  833.5 3.8 convolution_convert_fusion
  837.6 12.6 fusion
  850.3 1.9 slice-done.2
  853.1 7.5 fusion.2
  860.6 3.7 fusion.10
  864.6 9.9 dynamic_update_slice.22
  875.8 7.0 fusion.6
  883.0 10.8 dynamic_update_slice.23
  895.3 13.0 fusion.56
  908.6 12.7 fusion.57
  921.4 12.6 fusion.55
  935.1 4.4 multiply_convert_fusion.3
  942.3 5.0 fusion.51
  949.0 3.0 convolution_add_fusion.2
  952.1 9.4 reduce-scatter.18.cloned.1.call-done
  961.5 1.9 convolution_add_fusion.1
  968.9 2.3 fusion.34
  971.2 3.0 reshape.290
  974.2 2.8 copy.131
  977.3 2.3 copy.132
  979.6 6.4 fusion.54
  986.1 6.2 fusion.52
  993.0 44.6 %all-reduce.10 = (f32[1536]{0:T(1024)S(1)}, f32[1536]{0:T(1024)S(1)}, f32[256]{0:T(256)S(1)}, f32[256]{0:T(256)S(1)}, f32[1536]{0:T(1024)S(1)}) all-reduce(f32[1536]{0:T(1024)S(1)} %copy-done.35, f32[1536]{0:T(1024)S(1)} %bitcast.257, f32[256]{0:T(256)S(1)} %bitcast.261, ...), channel_id=10, replica_groups=mesh['row'=4,'col'=8] {'row','col'}, use_global_device_ids=true, to_apply=%region_15.16.clone | all-reduce | flops 5120 | bytes 40960
  1040.6 3.0 fusion.21
  1043.6 42.1 %reduce-scatter.28.cloned.1.call-done = f32[384,1120]{0,1:T(8,128)} async-done(((f32[1536,1120]{0,1:T(8,128)}), f32[384,1120]{0,1:T(8,128)}) %reduce-scatter.28.cloned.1.call-update) | async-done | bytes 1720336 | tf_op jit(solution)/shard_map/reduce_scatter | solution.py:364
  1085.7 123.6 %reduce-scatter.30.cloned.1.call-done = f32[384,1120]{0,1:T(8,128)} async-done(((f32[1536,1120]{0,1:T(8,128)}), f32[384,1120]{0,1:T(8,128)}) %reduce-scatter.30.cloned.1.call-update) | async-done | bytes 1720336 | tf_op jit(solution)/shard_map/reduce_scatter | solution.py:365
  1209.2 123.6 %reduce-scatter.32.cloned.1.call-done = f32[1120,384]{1,0:T(8,128)} async-done(((f32[1120,1536]{1,0:T(8,128)}), f32[1120,384]{1,0:T(8,128)}) %reduce-scatter.32.cloned.1.call-update) | async-done | bytes 1720336 | tf_op jit(solution)/shard_map/reduce_scatter | solution.py:366
  1332.9 104.1 %reduce-scatter.22.cloned.1.call-done = f32[1,384,32]{1,2,0:T(8,128)} async-done(((f32[32,384,32]{1,2,0:T(8,128)}), f32[1,384,32]{1,2,0:T(8,128)}) %reduce-scatter.22.cloned.1.call-update) | async-done | bytes 49168 | tf_op jit(solution)/shard_map/reduce_scatter | solution.py:334
  1437.0 102.6 %reduce-scatter.24.cloned.1.call-done = f32[1,384,32]{1,2,0:T(8,128)} async-done(((f32[32,384,32]{1,2,0:T(8,128)}), f32[1,384,32]{1,2,0:T(8,128)}) %reduce-scatter.24.cloned.1.call-update) | async-done | bytes 49168 | tf_op jit(solution)/shard_map/reduce_scatter | solution.py:340
  1539.6 141.7 %reduce-scatter.26.cloned.1.call-done = f32[1,384,192]{1,2,0:T(8,128)} async-done(((f32[32,384,192]{1,2,0:T(8,128)}), f32[1,384,192]{1,2,0:T(8,128)}) %reduce-scatter.26.cloned.1.call-update) | async-done | bytes 294928 | tf_op jit(solution)/shard_map/reduce_scatter | solution.py:346
  1681.3 141.4 %reduce-scatter.20.cloned.1.call-done = f32[1,384,192]{1,2,0:T(8,128)} async-done(((f32[32,384,192]{1,2,0:T(8,128)}), f32[1,384,192]{1,2,0:T(8,128)}) %reduce-scatter.20.cloned.1.call-update) | async-done | bytes 294928 | tf_op jit(solution)/shard_map/reduce_scatter | solution.py:328
  (225 shorter events, 57.8 us)
Async XLA Ops:
  7.2 92.2 %copy-start.1 = (bf16[256,1536]{1,0:T(8,128)(2,1)S(1)}, bf16[256,1536]{1,0:T(8,128)(2,1)}, u32[]{:S(2)}) copy-start(bf16[256,1536]{1,0:T(8,128)(2,1)} %param.15) | copy-start | bytes 2359300
  7.2 138.5 %all-gather.14.cloned.1.call-start = ((), (), s32[]{:S(2)}) async-start(), calls=%async_computation.11 | async-start | bytes 1179648 | tf_op jit(solution)/shard_map/all_gather | solution.py:181
  53.8 181.9 %copy-start.32 = (f32[1536]{0:T(1024)}, f32[1536]{0:T(1024)S(1)}, u32[]{:S(2)}) copy-start(f32[1536]{0:T(1024)S(1)} %convert_element_type.134) | copy-start | bytes 18436
  55.2 180.5 %copy-start.37 = (f32[256]{0:T(256)}, f32[256]{0:T(256)S(1)}, u32[]{:S(2)}) copy-start(f32[256]{0:T(256)S(1)} %add_rsqrt_fusion.1) | copy-start | bytes 3076
  97.9 2.6 copy-start.36
  100.4 39.6 %copy-start.40 = (s32[1,16]{1,0:T(1,128)S(1)}, s32[1,16]{1,0:T(1,128)}, u32[]{:S(2)}) copy-start(s32[1,16]{1,0:T(1,128)} %param.17) | copy-start | bytes 196
  100.5 62.8 %all-gather.16.cloned.1.call-start = ((), (), s32[]{:S(2)}) async-start(), calls=%async_computation.12 | async-start | bytes 1179648 | tf_op jit(solution)/shard_map/all_gather | solution.py:180
  140.0 4.6 copy-start.23
  141.0 3.7 copy-start.15
  141.0 159.3 %copy-start.13 = (f32[256,128]{0,1:T(8,128)}, f32[256,128]{0,1:T(8,128)S(1)}, u32[]{:S(2)}) copy-start(f32[256,128]{0,1:T(8,128)S(1)} %get-tuple-element.47) | copy-start | bytes 393220
  142.3 87.4 %all-gather.28.cloned.1.call-start = ((), (), s32[]{:S(2)}) async-start(), calls=%async_computation.29 | async-start | bytes 4866048 | tf_op jit(solution)/shard_map/all_gather | solution.py:114
  143.0 151.2 %all-gather.30.cloned.1.call-start = ((), (), s32[]{:S(2)}) async-start(), calls=%async_computation.30 | async-start | bytes 4866048 | tf_op jit(solution)/shard_map/all_gather | solution.py:117
  143.6 218.3 %all-gather.20.cloned.1.call-start = ((), (), s32[]{:S(2)}) async-start(), calls=%async_computation.14 | async-start | bytes 4300800 | tf_op jit(solution)/shard_map/all_gather | solution.py:141
  144.2 264.0 %all-gather.18.cloned.1.call-start = ((), (), s32[]{:S(2)}) async-start(), calls=%async_computation.13 | async-start | bytes 7077888 | tf_op jit(solution)/shard_map/all_gather | solution.py:214
  164.6 136.6 %copy-start.8 = (bf16[1280,256]{0,1:T(8,128)(2,1)}, bf16[1280,256]{0,1:T(8,128)(2,1)S(1)}, u32[]{:S(2)}) copy-start(bf16[1280,256]{0,1:T(8,128)(2,1)S(1)} %constant_dynamic-slice_fusion) | copy-start | bytes 1966084
  235.7 2.1 copy-start.10
  299.4 1.3 copy-start.21
  299.4 1.6 copy-start.22
  300.2 32.6 %copy-start.11 = (bf16[192,8,4,384]{3,1,2,0:T(8,128)(2,1)}, bf16[192,8,4,384]{3,1,2,0:T(8,128)(2,1)S(1)}, u32[]{:S(2)}) copy-start(bf16[192,8,4,384]{3,1,2,0:T(8,128)(2,1)S(1)} %copy.164) | copy-start | bytes 14155780
  301.2 16.6 copy-start.3
  317.8 7.7 copy-start.26
  332.8 1.6 copy-start.31
  335.5 142.4 %all-gather.22.cloned.1.call-start = ((), (), s32[]{:S(2)}) async-start(), calls=%async_computation.15 | async-start | bytes 4300800 | tf_op jit(solution)/shard_map/all_gather | solution.py:142
  336.3 209.9 %all-gather.26.cloned.1.call-start = ((), (), s32[]{:S(2)}) async-start(), calls=%async_computation.18 | async-start | bytes 4300800 | tf_op jit(solution)/shard_map/all_gather | solution.py:249
  337.0 255.0 %all-gather.24.cloned.1.call-start = ((), (), s32[]{:S(2)}) async-start(), calls=%async_computation.17 | async-start | bytes 7077888 | tf_op jit(solution)/shard_map/all_gather | solution.py:251
  337.7 395.0 %reduce-scatter.14.cloned.1.call-start = ((), (), s32[]{:S(2)}) async-start(), calls=%async_computation.19 | async-start | bytes 14155776 | tf_op jit(solution)/shard_map/reduce_scatter | solution.py:260
  592.1 20.8 %copy-start.43 = (bf16[1536,1120]{0,1:T(8,128)(2,1)S(1)}, bf16[1536,1120]{0,1:T(8,128)(2,1)}, u32[]{:S(2)}) copy-start(bf16[1536,1120]{0,1:T(8,128)(2,1)} %all-gather.20.cloned.1.call-done) | copy-start | bytes 10321924
  612.8 13.4 copy-start.44
  612.8 13.4 copy-start.45
  640.3 1.2 copy-start.12
  640.3 188.3 %reduce-scatter.12.cloned.1.call-start = ((), (), s32[]{:S(2)}) async-start(), calls=%async_computation.16 | async-start | bytes 14155776 | tf_op jit(solution)/shard_map/reduce_scatter | solution.py:220
  641.4 23.1 %collective-permute-start = (bf16[1120,384]{1,0:T(8,128)(2,1)S(1)}, bf16[1120,384]{1,0:T(8,128)(2,1)S(1)}, u32[]{:S(2)}, u32[]{:S(2)}) collective-permute-start(bf16[1120,384]{1,0:T(8,128)(2,1)S(1)} %copy-done.12), channel_id=1, source_target_pairs={{0,8},{8,16},{16,24},{24,0},{1,9},{9,17},{17,25},{25,1},{2,10},{10... | collective-permute-start | bytes 2580488 | tf_op jit(solution)/shard_map/ppermute | solution.py:137
  665.4 22.3 %collective-permute-start.1 = (bf16[1120,384]{1,0:T(8,128)(2,1)S(1)}, bf16[1120,384]{1,0:T(8,128)(2,1)}, u32[]{:S(2)}, u32[]{:S(2)}) collective-permute-start(bf16[1120,384]{1,0:T(8,128)(2,1)S(1)} %collective-permute-done), channel_id=1, source_target_pairs={{0,8},{8,16},{16,24},{24,0},{1,9},{9,17},{17,25},{25,1},{2,10},{10... | collective-permute-start | bytes 2580488 | tf_op jit(solution)/shard_map/ppermute | solution.py:137
  687.7 21.7 %collective-permute-start.2 = (bf16[1120,384]{1,0:T(8,128)(2,1)}, bf16[1120,384]{1,0:T(8,128)(2,1)}, u32[]{:S(2)}, u32[]{:S(2)}) collective-permute-start(bf16[1120,384]{1,0:T(8,128)(2,1)} %collective-permute-done.1), channel_id=1, source_target_pairs={{0,8},{8,16},{16,24},{24,0},{1,9},{9,17},{17,25},{25,1},{2,10},{10... | collective-permute-start | bytes 2580488 | tf_op jit(solution)/shard_map/ppermute | solution.py:137
  687.7 1.2 copy-start.30
  688.0 22.8 %copy-start.46 = (bf16[2048,1120]{0,1:T(8,128)(2,1)S(1)}, bf16[2048,1120]{0,1:T(8,128)(2,1)}, u32[]{:S(2)}) copy-start(bf16[2048,1120]{0,1:T(8,128)(2,1)} %get-tuple-element.36) | copy-start | bytes 13762564
  722.0 106.6 %copy-start.18 = (bf16[256,1536]{1,0:T(8,128)(2,1)S(1)}, bf16[256,1536]{1,0:T(8,128)(2,1)}, u32[]{:S(2)}) copy-start(bf16[256,1536]{1,0:T(8,128)(2,1)} %param.16) | copy-start | bytes 2359300
  722.0 225.2 %reduce-scatter.16.cloned.1.call-start = ((), (), s32[]{:S(2)}) async-start(), calls=%async_computation.20 | async-start | bytes 2359296 | tf_op jit(solution)/shard_map/reduce_scatter | solution.py:301
  833.5 4.1 copy-start.27
  837.6 12.7 slice-start
  837.6 12.7 slice-start.1
  837.6 14.6 slice-start.2
  837.6 15.5 slice-start.3
  853.1 7.5 copy-start.4
  860.6 3.7 copy-start
  874.4 1.3 copy-start.6
  875.8 85.7 %reduce-scatter.18.cloned.1.call-start = ((), (), s32[]{:S(2)}) async-start(), calls=%async_computation.21 | async-start | bytes 2359296 | tf_op jit(solution)/shard_map/reduce_scatter | solution.py:302
  893.9 1.4 copy-start.5
  895.3 190.4 %reduce-scatter.28.cloned.1.call-start = ((), (), s32[]{:S(2)}) async-start(), calls=%async_computation.26 | async-start | bytes 8601600 | tf_op jit(solution)/shard_map/reduce_scatter | solution.py:364
  908.3 300.9 %reduce-scatter.30.cloned.1.call-start = ((), (), s32[]{:S(2)}) async-start(), calls=%async_computation.27 | async-start | bytes 8601600 | tf_op jit(solution)/shard_map/reduce_scatter | solution.py:365
  921.3 411.5 %reduce-scatter.32.cloned.1.call-start = ((), (), s32[]{:S(2)}) async-start(), calls=%async_computation.28 | async-start | bytes 8601600 | tf_op jit(solution)/shard_map/reduce_scatter | solution.py:366
  934.0 5.5 copy-start.17
  934.0 502.9 %reduce-scatter.22.cloned.1.call-start = ((), (), s32[]{:S(2)}) async-start(), calls=%async_computation.23 | async-start | bytes 1622016 | tf_op jit(solution)/shard_map/reduce_scatter | solution.py:334
  942.3 6.8 copy-start.24
  947.2 14.3 copy-start.20
  949.0 14.4 copy-start.2
  949.0 14.4 copy-start.33
  949.0 14.4 copy-start.38
  964.6 4.3 copy-start.28
  968.8 570.8 %reduce-scatter.24.cloned.1.call-start = ((), (), s32[]{:S(2)}) async-start(), calls=%async_computation.24 | async-start | bytes 1622016 | tf_op jit(solution)/shard_map/reduce_scatter | solution.py:340
  977.0 704.3 %reduce-scatter.26.cloned.1.call-start = ((), (), s32[]{:S(2)}) async-start(), calls=%async_computation.25 | async-start | bytes 9732096 | tf_op jit(solution)/shard_map/reduce_scatter | solution.py:346
  986.1 836.7 %reduce-scatter.20.cloned.1.call-start = ((), (), s32[]{:S(2)}) async-start(), calls=%async_computation.22 | async-start | bytes 9732096 | tf_op jit(solution)/shard_map/reduce_scatter | solution.py:328
  992.3 48.3 %copy-start.41 = (f32[256]{0:T(256)S(1)}, f32[256]{0:T(256)}, u32[]{:S(2)}) copy-start(f32[256]{0:T(256)} %get-tuple-element.17) | copy-start | bytes 3076
  992.3 48.3 %copy-start.39 = (f32[256]{0:T(256)S(1)}, f32[256]{0:T(256)}, u32[]{:S(2)}) copy-start(f32[256]{0:T(256)} %copy-done.37) | copy-start | bytes 3076
  (10 other events, 8.9 us)
Sparse Core Ops, SparseCore 0:
  100.6 21.2 all-gather.13
  142.4 20.8 all-gather.15
  166.0 63.5 all-gather.27
  232.3 61.8 all-gather.29
  295.6 66.2 all-gather.19
  364.2 43.9 all-gather.17
  409.8 68.0 all-gather.21
  479.5 66.6 all-gather.25
  548.1 43.9 all-gather.23
  640.4 92.2 reduce-scatter.13
  736.2 92.2 reduce-scatter.11
  875.9 41.1 reduce-scatter.15
  920.3 41.1 reduce-scatter.17
  964.2 121.3 reduce-scatter.27
  1088.4 120.7 reduce-scatter.29
  1212.0 120.8 reduce-scatter.31
  1338.5 98.3 reduce-scatter.21
  1442.6 96.9 reduce-scatter.23
  1546.1 135.1 reduce-scatter.25
  1687.6 135.0 reduce-scatter.19
